TPU v7x, 32 devices: a whole 2x2x4 slice. The times are simulated.
32 devices in a mesh: grp: 2 (over y), hist: 4 (over z), chan: 2 (over x), seq: 2 (over core).
Axes of the slice: x: 2, y: 2, z: 4, core: 2. Of those that a mesh axis runs over, the one named last changes fastest.
Arguments:
- history: bfloat16 [16, 2048, 4096], P(('grp', 'seq'), 'hist', 'chan'), parts along dimension 0, may hold values from -6 to 6
- filter_taps: bfloat16 [4096, 4096], P(('grp', 'hist'), 'chan'), parts along dimension 0, may hold values from -0.125 to 0.125
- skip_gain: float32 [8192], P(('grp', 'chan')), parts along dimension 0, may hold values from -4 to 4
- gate_values: bfloat16 [16, 64, 4096], P(('grp', 'seq'), 'hist', 'chan'), parts along dimension 0, may hold values from -6 to 6
Outputs:
- output: bfloat16 [16, 64, 4096], P(('grp', 'seq'), 'hist', 'chan'), parts along dimension 0
There are 2 independent parts, one for each index of `grp`. A program takes and returns all parts, laid end to end along the dimension named above; each array names one. Nothing has to cross between parts.
All inputs are finite; a program needn't handle non-finite values.
Results may differ from a plain program's by a relative error of at most 0.0085.
Values may be sent and summed in bfloat16 or wider, within the bound.
A program may use at most 192 MiB of HBM per device.

v0:
```python
import math

import jax
import jax.numpy as jnp
from jax import lax
from jax.sharding import PartitionSpec as P

NEW = 64


def from_behind(value, axis, steps):
    count = lax.axis_size(axis)
    first, last = (max(0, -steps), min(count, count - steps))
    return lax.ppermute(value, axis, [(source, source + steps) for source in range(first, last)])


def phase_table(rows, length):
    row_ids = lax.iota(jnp.int32, rows)[:, None]
    col_ids = lax.iota(jnp.int32, length)[None, :]
    phase = row_ids * col_ids % length
    angle = 2.0 * math.pi / length * phase.astype(jnp.float32)
    return (jnp.cos(angle), jnp.sin(angle))


def split_table(table):
    upper = table.astype(jnp.bfloat16)
    lower = (table - upper.astype(jnp.float32)).astype(jnp.bfloat16)
    return (upper, lower)


def forward(data, table, form):
    upper, lower = table
    first = jnp.einsum(form, data, upper, preferred_element_type=jnp.float32)
    return first + jnp.einsum(form, data, lower, preferred_element_type=jnp.float32)


def inverse(spectra, table):
    data_upper, data_lower = split_table(spectra)
    table_upper, table_lower = table
    value = jnp.einsum("kc,ki->ic", data_upper, table_upper, preferred_element_type=jnp.float32)
    value = value + jnp.einsum(
        "kc,ki->ic", data_upper, table_lower, preferred_element_type=jnp.float32
    )
    return value + jnp.einsum(
        "kc,ki->ic", data_lower, table_upper, preferred_element_type=jnp.float32
    )


def body(history, filter_taps, skip_gain, gate_values):
    hist_count = lax.axis_size("hist")
    hist_index = lax.axis_index("hist")
    block_rows = history.shape[1]
    channels = history.shape[2]
    seq_count = history.shape[0]
    length = 2 * NEW
    groups = block_rows // NEW
    tap_rim = from_behind(filter_taps[:NEW], "hist", -1)
    extended = jnp.concatenate([filter_taps, tap_rim], axis=0)
    tap_blocks = jnp.concatenate(
        [
            extended[:block_rows].reshape(groups, NEW, channels),
            extended[NEW:].reshape(groups, NEW, channels),
        ],
        axis=1,
    )
    long_cos, long_sin = phase_table(length, length)
    short_cos, short_sin = phase_table(NEW, length)
    taps_cos = forward(tap_blocks, split_table(long_cos), "qsc,sk->qkc")
    taps_sin = forward(tap_blocks, split_table(long_sin), "qsc,sk->qkc")
    short_cos_parts = split_table(short_cos)
    short_sin_parts = split_table(short_sin)
    freq_ids = lax.iota(jnp.int32, length)[:, None]
    lag_ids = (NEW - 1 - lax.iota(jnp.int32, NEW))[None, :]
    back_angle = 2.0 * math.pi / length * (freq_ids * lag_ids % length).astype(jnp.float32)
    back_table = jnp.concatenate(
        [jnp.cos(back_angle) / length, -jnp.sin(back_angle) / length], axis=0
    )
    back_parts = split_table(back_table)
    rows_out = []
    for seq_id in range(seq_count):
        blocks_in = history[seq_id].reshape(groups, NEW, channels)
        input_cos = forward(blocks_in, short_cos_parts, "qrc,rk->qkc")
        input_sin = forward(blocks_in, short_sin_parts, "qrc,rk->qkc")
        real_part = jnp.sum(input_cos * taps_cos + input_sin * taps_sin, axis=0)
        imag_part = jnp.sum(input_sin * taps_cos - input_cos * taps_sin, axis=0)
        spectra = jnp.concatenate([real_part, imag_part], axis=0)
        rows_out.append(inverse(spectra, back_parts))
    partial_value = jnp.stack(rows_out, axis=0)
    newest_rows = history[:, block_rows - NEW :, :]
    last_flag = (hist_index == hist_count - 1).astype(jnp.float32)
    partial_value = partial_value + last_flag * skip_gain[None, None, :] * newest_rows.astype(
        jnp.float32
    )
    result = lax.psum_scatter(partial_value, "hist", scatter_dimension=1, tiled=True)
    return (gate_values.astype(jnp.float32) * result).astype(jnp.bfloat16)


def solution(mesh):
    placed = (
        P(("grp", "seq"), "hist", "chan"),
        P(("grp", "hist"), "chan"),
        P(("grp", "chan")),
        P(("grp", "seq"), "hist", "chan"),
    )
    return jax.shard_map(
        body,
        mesh=mesh,
        in_specs=placed,
        out_specs=P(("grp", "seq"), "hist", "chan"),
        check_vma=False,
    )
```

profile of v0, /device:TPU:0, one launch (start us, length us, event | category | flops | bytes accessed | tf_op | source)
XLA Modules:
  0.0 205.9 jit_solution(13798787908328344978)
XLA Ops:
  6.5 0.0 reduce-scatter.2.cloned.1.call-start
  6.5 1.0 slice.22
  7.5 1.3 collective-permute-start
  8.8 3.7 %fusion.192 = (bf16[1,512,2048]{2,1,0:T(8,128)(2,1)S(1)}, bf16[1,512,2048]{2,1,0:T(8,128)(2,1)S(1)}, bf16[1,512,2048]{2,1,0:T(8,128)(2,1)S(1)}, bf16[1,512,2048]{2,1,0:T(8,128)(2,1)S(1)}) fusion(bf16[4,512,2048]{2,1,0:T(8,128)(2,1)} %param.4), kind=kLoop, calls=%fused_computation.212 | loop fusion | bytes 16777216 | tf_op jit(solution)/shard_map/slice | solution.py:81
  12.6 4.7 %fusion.63 = f32[128,8,2048]{2,0,1:T(8,128)} fusion(bf16[8,64,2048]{2,1,0:T(8,128)(2,1)S(1)} %bitcast.106), kind=kOutput, calls=%fused_computation.98 | convolution fusion | flops 268558336 | bytes 10485760 | tf_op jit(solution)/shard_map/qrc,rk->qkc/dot_general | solution.py:33
  17.3 4.6 %fusion.71 = f32[128,8,2048]{2,0,1:T(8,128)} fusion(bf16[8,64,2048]{2,1,0:T(8,128)(2,1)S(1)} %bitcast.107), kind=kOutput, calls=%fused_computation.106 | convolution fusion | flops 268558336 | bytes 10485760 | tf_op jit(solution)/shard_map/qrc,rk->qkc/dot_general | solution.py:33
  21.9 4.6 %fusion.65 = f32[128,8,2048]{2,0,1:T(8,128)} fusion(bf16[8,64,2048]{2,1,0:T(8,128)(2,1)S(1)} %bitcast.102), kind=kOutput, calls=%fused_computation.100 | convolution fusion | flops 268558336 | bytes 10485760 | tf_op jit(solution)/shard_map/qrc,rk->qkc/dot_general | solution.py:33
  26.5 4.6 %fusion.73 = f32[128,8,2048]{2,0,1:T(8,128)} fusion(bf16[8,64,2048]{2,1,0:T(8,128)(2,1)S(1)} %bitcast.103), kind=kOutput, calls=%fused_computation.108 | convolution fusion | flops 268558336 | bytes 10485760 | tf_op jit(solution)/shard_map/qrc,rk->qkc/dot_general | solution.py:33
  31.1 4.6 %fusion.67 = f32[128,8,2048]{2,0,1:T(8,128)} fusion(bf16[8,64,2048]{2,1,0:T(8,128)(2,1)S(1)} %bitcast.94), kind=kOutput, calls=%fused_computation.102 | convolution fusion | flops 268558336 | bytes 10485760 | tf_op jit(solution)/shard_map/qrc,rk->qkc/dot_general | solution.py:33
  35.7 1.4 fusion.75
  37.1 1.4 fusion.77
  38.5 1.4 fusion.69
  39.9 8.1 %convolution_add_fusion = f32[128,8,2048]{2,0,1:T(8,128)} fusion(f32[128,8,2048]{2,0,1:T(8,128)} %fusion.63, bf16[8,64,2048]{2,1,0:T(8,128)(2,1)S(1)} %bitcast.108), kind=kOutput, calls=%fused_computation.8 | convolution fusion | flops 270680064 | bytes 18874368 | tf_op jit(solution)/shard_map/qrc,rk->qkc/dot_general | solution.py:34
  48.1 8.2 %convolution_add_fusion.1 = f32[128,8,2048]{2,0,1:T(8,128)} fusion(f32[128,8,2048]{2,0,1:T(8,128)} %fusion.71, bf16[8,64,2048]{2,1,0:T(8,128)(2,1)S(1)} %bitcast.109), kind=kOutput, calls=%fused_computation.9 | convolution fusion | flops 270680064 | bytes 18874368 | tf_op jit(solution)/shard_map/qrc,rk->qkc/dot_general | solution.py:34
  56.3 8.0 %convolution_add_fusion.2 = f32[128,8,2048]{2,0,1:T(8,128)} fusion(f32[128,8,2048]{2,0,1:T(8,128)} %fusion.65, bf16[8,64,2048]{2,1,0:T(8,128)(2,1)S(1)} %bitcast.104), kind=kOutput, calls=%fused_computation.10 | convolution fusion | flops 270680064 | bytes 18874368 | tf_op jit(solution)/shard_map/qrc,rk->qkc/dot_general | solution.py:34
  64.3 8.0 %convolution_add_fusion.3 = f32[128,8,2048]{2,0,1:T(8,128)} fusion(f32[128,8,2048]{2,0,1:T(8,128)} %fusion.73, bf16[8,64,2048]{2,1,0:T(8,128)(2,1)S(1)} %bitcast.105), kind=kOutput, calls=%fused_computation.11 | convolution fusion | flops 270680064 | bytes 18874368 | tf_op jit(solution)/shard_map/qrc,rk->qkc/dot_general | solution.py:34
  72.3 8.0 %convolution_add_fusion.4 = f32[128,8,2048]{2,0,1:T(8,128)} fusion(f32[128,8,2048]{2,0,1:T(8,128)} %fusion.67, bf16[8,64,2048]{2,1,0:T(8,128)(2,1)S(1)} %bitcast.96), kind=kOutput, calls=%fused_computation.12 | convolution fusion | flops 270680064 | bytes 18874368 | tf_op jit(solution)/shard_map/qrc,rk->qkc/dot_general | solution.py:34
  80.3 4.6 %convolution_add_fusion.5 = f32[128,8,2048]{2,0,1:T(8,128)} fusion(f32[128,8,2048]{2,0,1:T(8,128)S(1)} %fusion.75, bf16[8,64,2048]{2,1,0:T(8,128)(2,1)S(1)} %bitcast.97), kind=kOutput, calls=%fused_computation.13 | convolution fusion | flops 270680064 | bytes 18874368 | tf_op jit(solution)/shard_map/qrc,rk->qkc/dot_general | solution.py:34
  84.9 4.6 %convolution_add_fusion.7 = f32[128,8,2048]{2,0,1:T(8,128)} fusion(f32[128,8,2048]{2,0,1:T(8,128)S(1)} %fusion.77, bf16[8,64,2048]{2,1,0:T(8,128)(2,1)S(1)} %bitcast.92), kind=kOutput, calls=%fused_computation.15 | convolution fusion | flops 270680064 | bytes 18874368 | tf_op jit(solution)/shard_map/qrc,rk->qkc/dot_general | solution.py:34
  89.6 0.0 copy-start.10
  89.6 0.0 copy-start
  89.6 4.6 %convolution_add_fusion.6 = f32[128,8,2048]{2,0,1:T(8,128)} fusion(f32[128,8,2048]{2,0,1:T(8,128)S(1)} %fusion.69, bf16[8,64,2048]{2,1,0:T(8,128)(2,1)S(1)} %bitcast.93), kind=kOutput, calls=%fused_computation.14 | convolution fusion | flops 270680064 | bytes 18874368 | tf_op jit(solution)/shard_map/qrc,rk->qkc/dot_general | solution.py:34
  94.2 0.2 cosine_multiply_fusion
  94.4 0.0 copy-done.10
  94.5 0.0 collective-permute-done
  94.5 0.0 copy-done
  94.5 0.2 pad_maximum_fusion.1
  94.7 0.0 copy-start.1
  94.7 1.5 fusion.43
  96.2 4.7 %fusion.41 = f32[128,8,2048]{2,0,1:T(8,128)} fusion(bf16[8,64,2048]{2,1,0:T(8,128)(2,1)S(1)} %bitcast.99, bf16[8,64,2048]{2,1,0:T(8,128)(2,1)S(1)} %bitcast.87), kind=kOutput, calls=%fused_computation.78 | convolution fusion | flops 545505280 | bytes 12582912 | tf_op jit(solution)/shard_map/qsc,sk->qkc/dot_general | solution.py:33
  100.9 0.0 copy-done.1
  100.9 4.2 %convolution_add_fusion.9 = f32[128,8,2048]{2,0,1:T(8,128)} fusion(f32[128,8,2048]{2,0,1:T(8,128)S(1)} %fusion.43, bf16[8,64,2048]{2,1,0:T(8,128)(2,1)S(1)} %bitcast.100, bf16[8,64,2048]{2,1,0:T(8,128)(2,1)S(1)} %bitcast.88), kind=kOutput, calls=%fused_computation.17 | convolution fusion | flops 547651584 | bytes 20971520 | tf_op jit(solution)/shard_map/qsc,sk->qkc/dot_general | solution.py:34
  105.1 32.8 %add_reduce_fusion.3 = (f32[128,2048]{1,0:T(8,128)}, f32[128,2048]{1,0:T(8,128)}, f32[128,2048]{1,0:T(8,128)S(1)}, f32[128,2048]{1,0:T(8,128)}, f32[128,2048]{1,...) fusion(f32[128,8,2048]{2,0,1:T(8,128)} %convolution_add_fusion.6, ...), kind=kOutput, calls=%fused_computation.7 | convolution fusion | flops 612663296 | bytes 96468992 | tf_op jit(solution)/shard_map/qsc,sk->qkc/dot_general | solution.py:34
  137.8 0.0 copy-start.7
  137.8 2.0 fusion.10
  139.8 0.0 copy-done.7
  139.8 0.2 copy-done.8
  140.0 0.3 convolution_add_fusion.17
  140.3 0.0 copy-start.5
  140.3 0.0 copy-start.6
  140.3 0.3 fusion
  140.6 0.9 copy-done.5
  141.5 0.3 copy-done.6
  141.8 0.3 fusion.14
  142.1 0.3 convolution_add_fusion.15
  142.5 0.0 copy-start.3
  142.5 0.0 copy-start.4
  142.5 0.3 fusion.1
  142.8 0.9 copy-done.3
  143.7 0.3 copy-done.4
  144.0 0.3 fusion.18
  144.3 0.3 convolution_add_fusion.13
  144.6 0.0 copy-start.2
  144.6 0.3 fusion.2
  144.9 0.9 copy-done.2
  145.8 0.3 fusion.22
  146.1 0.3 convolution_add_fusion.11
  146.4 0.3 fusion.3
  146.8 2.9 %maximum_add_fusion = f32[4,64,2048]{2,1,0:T(8,128)} fusion(f32[1,64,2048]{2,1,0:T(8,128)S(1)} %fusion.3, f32[1,64,2048]{2,1,0:T(8,128)S(1)} %fusion.2, f32[1,64,2048]{2,1,0:T(8,128)S(1)} %fusion.1, f32[1,64,2048]{2,1,0:T(8,128)S(1)} %fusion, bf16[4,512,2048]{2,1,0:T(8,128)(2,1)} %param.4, f32[2048]{0:T(1024)S(1)} %broadcast_multiply_fusion), kind=kLoop, calls=%fused_computation.36 | loop fusion | flops 3145728 | bytes 5251072 | tf_op jit(solution)/shard_map/add | solution.py:91
  149.7 0.0 copy-start.9
  149.7 0.0 reduce-scatter.2.cloned.1.call-update
  149.7 47.6 %reduce-scatter.2.cloned.1.call-done = f32[4,16,2048]{2,1,0:T(8,128)} async-done(((f32[4,64,2048]{2,1,0:T(8,128)}), f32[4,16,2048]{2,1,0:T(8,128)}) %reduce-scatter.2.cloned.1.call-update) | async-done | bytes 524304 | tf_op jit(solution)/shard_map/reduce_scatter | solution.py:94
  197.3 0.0 copy-done.9
  197.3 1.8 multiply_convert_fusion
  (4 shorter events, 0.0 us)
Async XLA Ops:
  6.5 190.7 %reduce-scatter.2.cloned.1.call-start = ((), (), s32[]{:S(2)}) async-start(), calls=%async_computation.1 | async-start | bytes 2621440 | tf_op jit(solution)/shard_map/reduce_scatter | solution.py:94
  7.5 87.0 %collective-permute-start = (bf16[64,2048]{1,0:T(8,128)(2,1)S(1)}, bf16[64,2048]{1,0:T(8,128)(2,1)S(1)}, u32[]{:S(2)}, u32[]{:S(2)}) collective-permute-start(bf16[64,2048]{1,0:T(8,128)(2,1)S(1)} %slice.22), channel_id=1, source_target_pairs={{4,0},{8,4},{12,8},{5,1},{9,5},{13,9},{6,2},{10,6},{14,10},{7,3},{... | collective-permute-start | bytes 786440 | tf_op jit(solution)/shard_map/ppermute | solution.py:14
  89.6 4.9 %copy-start.10 = (f32[2048]{0:T(1024)S(1)}, f32[2048]{0:T(1024)}, u32[]{:S(2)}) copy-start(f32[2048]{0:T(1024)} %param.6) | copy-start | bytes 24580
  89.6 4.9 %copy-start = (bf16[512,2048]{1,0:T(8,128)(2,1)S(1)}, bf16[512,2048]{1,0:T(8,128)(2,1)}, u32[]{:S(2)}) copy-start(bf16[512,2048]{1,0:T(8,128)(2,1)} %param.5) | copy-start | bytes 6291460
  94.7 6.2 %copy-start.1 = (bf16[512,2048]{1,0:T(8,128)(2,1)}, bf16[512,2048]{1,0:T(8,128)(2,1)S(1)}, u32[]{:S(2)}) copy-start(bf16[512,2048]{1,0:T(8,128)(2,1)S(1)} %pad_maximum_fusion.1) | copy-start | bytes 6291460
  137.8 2.0 copy-start.7
  137.8 2.2 %copy-start.8 = (f32[128,2048]{1,0:T(8,128)S(1)}, f32[128,2048]{1,0:T(8,128)}, u32[]{:S(2)}) copy-start(f32[128,2048]{1,0:T(8,128)} %get-tuple-element.6) | copy-start | bytes 3145732
  140.3 1.2 copy-start.5
  140.3 1.5 copy-start.6
  142.5 1.2 copy-start.3
  142.5 1.5 copy-start.4
  144.6 1.2 copy-start.2
  149.7 47.6 %copy-start.9 = (bf16[4,16,2048]{2,1,0:T(8,128)(2,1)S(1)}, bf16[4,16,2048]{2,1,0:T(8,128)(2,1)}, u32[]{:S(2)}) copy-start(bf16[4,16,2048]{2,1,0:T(8,128)(2,1)} %param.7) | copy-start | bytes 786436
Sparse Core Ops, SparseCore 0:
  149.8 47.4 reduce-scatter.1
where the time goes:
time: 206 us
  matrix products  130 us (63%)
  waiting for transfers between devices  47.6 us (23%)
  between operations  13.6 us (7%)
  local copies, waits for them, and re-layouts  8.24 us (4%)
  other arithmetic  5.16 us (3%)
    dot_general x10, matrix products, forward(): jnp.einsum(form, data, lower, preferred_element_type=jnp.float32)  91.2 us
    reduce_scatter x1, waiting for transfers between devices, body(): lax.psum_scatter(partial_value, 'hist', scatter_dimension=1, tiled=True)  47.6 us
    dot_general x10, matrix products, forward(): first = jnp.einsum(form, data, upper, preferred_element_type=jnp.float32)  33.5 us
  transfers between devices with their start and end apart: 2, of which 1 were waited for; matrix products, arithmetic and copies ran while one was open for 42% of the time, Pallas kernels for 0%

commit v1 on v0

v1 whole, which is shorter than its diff:
```python
import functools
import math

import jax
import jax.numpy as jnp
import numpy as np
from jax import lax
from jax.experimental import pallas as pl
from jax.experimental.pallas import tpu as pltpu
from jax.sharding import PartitionSpec as P

MESH = pl.DeviceIdType.MESH
F32 = jnp.float32
BF16 = jnp.bfloat16
LAG = 2


def tables(new, piece):
    length = piece + new
    freqs = 2 * np.arange(length // 2)[:, None] + 1

    def both(times):
        angle = math.pi / length * (freqs * times[None, :] % (2 * length))
        return np.concatenate([np.cos(angle), np.sin(angle)], axis=0)

    taps_table = both(np.arange(length))
    data_table = both(np.arange(piece))
    back_table = both(new - 1 - np.arange(new)).T * (2.0 / length)
    return [jnp.asarray(table, BF16) for table in (taps_table, data_table, back_table)]


def kernel(
    n, new, piece, width, first,
    ft_hbm, fh_hbm, fi_hbm, hist_hbm, taps_hbm, gain_hbm, gate_hbm, out_hbm,
    ft, fh, fi, hist, taps, gain, gate, out, tspec, spec, part,
    send, recv, in_sem, small_sem, out_sem, rim_send, rim_recv, send_sem, recv_sem,
):
    me = lax.axis_index("hist")
    right, left = lax.rem(me + 1, n), lax.rem(me + n - 1, n)
    chunks, seqs, block, _ = hist.shape
    own = new // n
    half = n // 2
    bins = (piece + new) // 2
    pieces = block // piece

    def lanes(c):
        return pl.ds(pl.multiple_of(c * width, width), width)

    small = [
        pltpu.make_async_copy(source, target, small_sem.at[i])
        for i, (source, target) in enumerate(
            [(ft_hbm, ft), (fh_hbm, fh), (fi_hbm, fi), (gain_hbm, gain), (gate_hbm, gate)]
        )
    ]

    def load_taps(c):
        return pltpu.make_async_copy(
            taps_hbm.at[:, lanes(c)], taps.at[c, pl.ds(0, block)], in_sem.at[0, c]
        )

    def load_hist(c):
        return pltpu.make_async_copy(hist_hbm.at[:, :, lanes(c)], hist.at[c], in_sem.at[1, c])

    def store(c):
        return pltpu.make_async_copy(out.at[c], out_hbm.at[:, :, lanes(c)], out_sem.at[c])

    def rim_copy(c):
        return pltpu.make_async_remote_copy(
            src_ref=taps_hbm.at[pl.ds(0, new), lanes(c)],
            dst_ref=taps.at[c, pl.ds(block, new)],
            send_sem=rim_send.at[c],
            recv_sem=rim_recv.at[c],
            device_id={"hist": left},
            device_id_type=MESH,
        )

    def span(way, stage):
        if stage > 0:
            return 0, seqs
        return (0, first) if way == 0 else (first, seqs - first)

    def hop(way, stage, c):
        start, count = span(way, stage)
        return pltpu.make_async_remote_copy(
            src_ref=send.at[way, stage, c, pl.ds(start, count)],
            dst_ref=recv.at[way, stage, c, pl.ds(start, count)],
            send_sem=send_sem.at[way, stage, c],
            recv_sem=recv_sem.at[way, stage, c],
            device_id={"hist": right if way == 0 else left},
            device_id_type=MESH,
        )

    for copy in small[:3]:
        copy.start()

    def start_loads(c, carry):
        load_taps(c).start()
        load_hist(c).start()
        return carry

    lax.fori_loop(0, chunks, start_loads, 0)
    for copy in small[3:]:
        copy.start()

    barrier = pltpu.get_barrier_semaphore()
    for neighbour in (left, right):
        pl.semaphore_signal(barrier, inc=1, device_id={"hist": neighbour}, device_id_type=MESH)
    pl.semaphore_wait(barrier, 2)

    def start_rims(c, carry):
        rim_copy(c).start()
        return carry

    lax.fori_loop(0, chunks, start_rims, 0)
    for copy in small:
        copy.wait()
    last = (me == n - 1).astype(F32)
    inner = (me != n - 1).astype(F32)

    def compute(c):
        load_taps(c).wait()
        rim_copy(c).wait_recv()
        rim = taps[c, pl.ds(block, new)].astype(F32) * inner
        taps[c, pl.ds(block, new)] = rim.astype(BF16)
        for q in range(pieces):
            tspec[q] = jnp.dot(
                ft[...], taps[c, pl.ds(q * piece, piece + new)], preferred_element_type=F32
            )
        load_hist(c).wait()
        gains = gain[:, lanes(c)] * last
        for b in range(seqs):
            data = [
                jnp.dot(fh[...], hist[c, b, pl.ds(q * piece, piece)], preferred_element_type=F32)
                for q in range(pieces)
            ]
            for r in range(0, bins, 16):
                real = imag = None
                for q in range(pieces):
                    hc, hs = data[q][r : r + 16], data[q][bins + r : bins + r + 16]
                    tc, ts = tspec[q, pl.ds(r, 16)], tspec[q, pl.ds(bins + r, 16)]
                    one, two = tc * hc + ts * hs, ts * hc - tc * hs
                    real = one if q == 0 else real + one
                    imag = two if q == 0 else imag + two
                spec[b, pl.ds(r, 16)] = real.astype(BF16)
                spec[b, pl.ds(bins + r, 16)] = imag.astype(BF16)
            value = jnp.dot(fi[...], spec[b], preferred_element_type=F32)
            value = value + gains * hist[c, b, pl.ds(block - new, new)].astype(F32)
            for d in range(n):
                part[c, d, b] = value[d * own : (d + 1) * own]

    def pass_on(stage, c):
        for way in range(2):
            start, count = span(way, stage)
            if count == 0:
                continue
            ahead = half - stage
            owner = lax.rem(me + (ahead if way == 0 else n - ahead), n)
            before, size = span(way, stage - 1) if stage else (0, 0)
            if size:
                hop(way, stage - 1, c).wait_recv()
            for b in range(start, start + count):
                value = part[c, owner, b]
                if before <= b < before + size:
                    value = value + recv[way, stage - 1, c, b].astype(F32)
                send[way, stage, c, b] = value.astype(BF16)
            hop(way, stage, c).start()

    def finish(c):
        total = [part[c, me, b] for b in range(seqs)]
        for way in range(2):
            start, count = span(way, half - 1)
            if count == 0:
                continue
            hop(way, half - 1, c).wait_recv()
            for b in range(start, start + count):
                total[b] = total[b] + recv[way, half - 1, c, b].astype(F32)
        for b in range(seqs):
            out[c, b] = (gate[b, :, lanes(c)].astype(F32) * total[b]).astype(BF16)
        store(c).start()

    def step(i, carry):
        @pl.when(i < chunks)
        def _():
            compute(i)
            pass_on(0, i)

        for stage in range(1, half + 1):
            c = i - stage * LAG

            @pl.when(jnp.logical_and(c >= 0, c < chunks))
            def _():
                if stage < half:
                    pass_on(stage, c)
                else:
                    finish(c)

        return carry

    lax.fori_loop(0, chunks + half * LAG, step, 0)

    def drain(c, carry):
        store(c).wait()
        rim_copy(c).wait_send()
        for stage in range(half):
            for way in range(2):
                if span(way, stage)[1]:
                    hop(way, stage, c).wait_send()
        return carry

    lax.fori_loop(0, chunks, drain, 0)


def body(history, filter_taps, skip_gain, gate_values):
    n = lax.axis_size("hist")
    seqs, block, channels = history.shape
    own = gate_values.shape[1]
    new = own * n
    piece = min(2 * new, block)
    width = min(256, channels)
    chunks = channels // width
    half = n // 2
    length = piece + new
    first = (3 * seqs) // 4
    hbm = pl.BlockSpec(memory_space=pl.ANY)
    return pl.pallas_call(
        functools.partial(kernel, n, new, piece, width, first),
        out_shape=jax.ShapeDtypeStruct(gate_values.shape, BF16),
        in_specs=[hbm] * 7,
        out_specs=hbm,
        scratch_shapes=[
            pltpu.VMEM((length, length), BF16),
            pltpu.VMEM((length, piece), BF16),
            pltpu.VMEM((new, length), BF16),
            pltpu.VMEM((chunks, seqs, block, width), BF16),
            pltpu.VMEM((chunks, block + new, width), BF16),
            pltpu.VMEM((1, channels), F32),
            pltpu.VMEM(gate_values.shape, BF16),
            pltpu.VMEM((chunks, seqs, own, width), BF16),
            pltpu.VMEM((block // piece, length, width), F32),
            pltpu.VMEM((seqs, length, width), BF16),
            pltpu.VMEM((chunks, n, seqs, own, width), F32),
            pltpu.VMEM((2, half, chunks, seqs, own, width), BF16),
            pltpu.VMEM((2, half, chunks, seqs, own, width), BF16),
            pltpu.SemaphoreType.DMA((2, chunks)),
            pltpu.SemaphoreType.DMA((5,)),
            pltpu.SemaphoreType.DMA((chunks,)),
            pltpu.SemaphoreType.DMA((chunks,)),
            pltpu.SemaphoreType.DMA((chunks,)),
            pltpu.SemaphoreType.DMA((2, half, chunks)),
            pltpu.SemaphoreType.DMA((2, half, chunks)),
        ],
        compiler_params=pltpu.CompilerParams(
            collective_id=0, has_side_effects=True, vmem_limit_bytes=48 * 1024 * 1024
        ),
    )(*tables(new, piece), history, filter_taps, skip_gain[None, :], gate_values)


def solution(mesh):
    placed = (
        P(("grp", "seq"), "hist", "chan"),
        P(("grp", "hist"), "chan"),
        P(("grp", "chan")),
        P(("grp", "seq"), "hist", "chan"),
    )
    return jax.shard_map(
        body,
        mesh=mesh,
        in_specs=placed,
        out_specs=P(("grp", "seq"), "hist", "chan"),
        check_vma=False,
    )
```

time: 206 us -> 40.2 us (0.20)
  matrix products: 130 us -> 0 us
  waiting for transfers between devices: 47.6 us -> 0 us
  Pallas kernels: 0 us -> 33.5 us
  between operations: 13.6 us -> 0.02 us
  other arithmetic: 5.16 us -> 0 us
    dot_general x32 -> x0, matrix products: 130 us -> none  [the longest x10 91.2 us: forward(): jnp.einsum(form, data, lower, preferred_element_type=jnp.float32)]
    reduce_scatter x1 -> x0, waiting for transfers between devices: 47.6 us -> none  [body(): lax.psum_scatter(partial_value, 'hist', scatter_dimension=1, tiled=True)]
    pallas_call x0 -> x1, Pallas kernels: none -> 33.5 us  [body(): pl.pallas_call(functools.partial(kernel, n, new, piece, width, first), ou...]
    slice x2 -> x0, local copies, waits for them, and re-layouts: 4.71 us -> none  [the longest x1 3.74 us: body(): blocks_in = history[seq_id].reshape(groups, NEW, channels)]
    add x1 -> x0, other arithmetic: 2.91 us -> none  [body(): partial_value + last_flag * skip_gain[None, None, :] * newest_rows.astype...]
    unnamed x22 -> x13, local copies, waits for them, and re-layouts: 3.53 us -> 6.39 us
  transfers between devices with their start and end apart: 2 -> 0, of which waited for: 1 -> 0; matrix products, arithmetic and copies ran while one was open for 42% -> 0% of each run, Pallas kernels for 0% -> 0%
where the time goes in v1:
time: 40.2 us; the launch traced here: 39.9 us
  Pallas kernels  33.5 us (83%)
  local copies, waits for them, and re-layouts  6.39 us (16%)
    pallas_call x1, Pallas kernels, body(): pl.pallas_call(functools.partial(kernel, n, new, piece, width, first), ou...  33.5 us
    unnamed x13, local copies, waits for them, and re-layouts  6.39 us

profile of v1, /device:TPU:0, one launch (start us, length us, event | category | flops | bytes accessed | tf_op | source)
XLA Modules:
  0.0 39.9 jit_solution(5689968184328075239)
XLA Ops:
  0.0 0.0 copy-start
  0.0 1.6 %copy-done = bf16[512,2048]{1,0:T(8,128)(2,1)S(1)} copy-done((bf16[512,2048]{1,0:T(8,128)(2,1)S(1)}, bf16[512,2048]{1,0:T(8,128)(2,1)}, u32[]{:S(2)}) %copy-start) | copy-done | bytes 2097176
  1.6 0.0 copy-start.1
  1.6 0.9 %copy-done.1 = bf16[4,16,2048]{2,1,0:T(8,128)(2,1)S(1)} copy-done((bf16[4,16,2048]{2,1,0:T(8,128)(2,1)S(1)}, bf16[4,16,2048]{2,1,0:T(8,128)(2,1)}, u32[]{:S(2)}) %copy-start.1) | copy-done | bytes 262168
  2.5 0.0 copy-start.2
  2.5 0.9 %copy-done.2 = bf16[192,192]{1,0:T(8,128)(2,1)S(1)} copy-done((bf16[192,192]{1,0:T(8,128)(2,1)S(1)}, bf16[192,192]{1,0:T(8,128)(2,1)}, u32[]{:S(2)}) %copy-start.2) | copy-done | bytes 73752
  3.4 0.0 copy-start.3
  3.4 0.8 %copy-done.3 = bf16[192,128]{1,0:T(8,128)(2,1)S(1)} copy-done((bf16[192,128]{1,0:T(8,128)(2,1)S(1)}, bf16[192,128]{1,0:T(8,128)(2,1)}, u32[]{:S(2)}) %copy-start.3) | copy-done | bytes 49176
  4.2 0.0 copy-start.4
  4.2 0.8 %copy-done.4 = bf16[64,192]{1,0:T(8,128)(2,1)S(1)} copy-done((bf16[64,192]{1,0:T(8,128)(2,1)S(1)}, bf16[64,192]{1,0:T(8,128)(2,1)}, u32[]{:S(2)}) %copy-start.4) | copy-done | bytes 24600
  5.0 0.0 copy-start.5
  5.0 0.7 %copy-done.5 = f32[2048]{0:T(1024)S(1)} copy-done((f32[2048]{0:T(1024)S(1)}, f32[2048]{0:T(1024)}, u32[]{:S(2)}) %copy-start.5) | copy-done | bytes 8216
  5.7 33.5 %shard_map.73 = bf16[4,16,2048]{2,1,0:T(8,128)(2,1)S(1)} custom-call(bf16[192,192]{1,0:T(8,128)(2,1)S(1)} %copy-done.2, bf16[192,128]{1,0:T(8,128)(2,1)S(1)} %copy-done.3, bf16[64,192]{1,0:T(8,128)(2,1)S(1)} %copy-done.4, bf16[4,512,2048]{2,1,0:T(8,128)(2,1)} %hist_hbm.1, bf16[512,2048]{1,0:T(8,128)(2,1)S(1)} %copy-done, f32[1,2048]{1,0:T(1,128)S(1)} %bitcast.1, ...), custom_call_target="tpu_custom_call" | custom-call | tf_op jit(solution)/shard_map/pallas_call | solution.py:225
  39.2 0.7 %copy.9 = bf16[4,16,2048]{2,1,0:T(8,128)(2,1)} copy(bf16[4,16,2048]{2,1,0:T(8,128)(2,1)S(1)} %shard_map.73) | data formatting | bytes 524288
Async XLA Ops:
  0.0 1.6 %copy-start = (bf16[512,2048]{1,0:T(8,128)(2,1)S(1)}, bf16[512,2048]{1,0:T(8,128)(2,1)}, u32[]{:S(2)}) copy-start(bf16[512,2048]{1,0:T(8,128)(2,1)} %taps_hbm.1) | copy-start | bytes 6291460
  1.6 0.9 %copy-start.1 = (bf16[4,16,2048]{2,1,0:T(8,128)(2,1)S(1)}, bf16[4,16,2048]{2,1,0:T(8,128)(2,1)}, u32[]{:S(2)}) copy-start(bf16[4,16,2048]{2,1,0:T(8,128)(2,1)} %gate_hbm.1) | copy-start | bytes 786436
  2.5 0.9 %copy-start.2 = (bf16[192,192]{1,0:T(8,128)(2,1)S(1)}, bf16[192,192]{1,0:T(8,128)(2,1)}, u32[]{:S(2)}) copy-start(bf16[192,192]{1,0:T(8,128)(2,1)} %constant.6.clone.ft_hbm) | copy-start | bytes 221188
  3.4 0.8 %copy-start.3 = (bf16[192,128]{1,0:T(8,128)(2,1)S(1)}, bf16[192,128]{1,0:T(8,128)(2,1)}, u32[]{:S(2)}) copy-start(bf16[192,128]{1,0:T(8,128)(2,1)} %constant.7.clone.fh_hbm) | copy-start | bytes 147460
  4.2 0.8 %copy-start.4 = (bf16[64,192]{1,0:T(8,128)(2,1)S(1)}, bf16[64,192]{1,0:T(8,128)(2,1)}, u32[]{:S(2)}) copy-start(bf16[64,192]{1,0:T(8,128)(2,1)} %constant.8.clone.fi_hbm) | copy-start | bytes 73732
  5.0 0.7 %copy-start.5 = (f32[2048]{0:T(1024)S(1)}, f32[2048]{0:T(1024)}, u32[]{:S(2)}) copy-start(f32[2048]{0:T(1024)} %param.9) | copy-start | bytes 24580

commit v2 on v1

--- a/solution.py
+++ b/solution.py
@@ -111,17 +111,25 @@
         rim_copy(c).start()
         return carry
 
-    lax.fori_loop(0, chunks, start_rims, 0)
+    @pl.when(me != 0)
+    def _():
+        lax.fori_loop(0, chunks, start_rims, 0)
+
     for copy in small:
         copy.wait()
     last = (me == n - 1).astype(F32)
-    inner = (me != n - 1).astype(F32)
 
     def compute(c):
         load_taps(c).wait()
-        rim_copy(c).wait_recv()
-        rim = taps[c, pl.ds(block, new)].astype(F32) * inner
-        taps[c, pl.ds(block, new)] = rim.astype(BF16)
+
+        @pl.when(me != n - 1)
+        def _():
+            rim_copy(c).wait_recv()
+
+        @pl.when(me == n - 1)
+        def _():
+            taps[c, pl.ds(block, new)] = jnp.zeros((new, width), BF16)
+
         for q in range(pieces):
             tspec[q] = jnp.dot(
                 ft[...], taps[c, pl.ds(q * piece, piece + new)], preferred_element_type=F32
@@ -200,7 +208,11 @@
 
     def drain(c, carry):
         store(c).wait()
-        rim_copy(c).wait_send()
+
+        @pl.when(me != 0)
+        def _():
+            rim_copy(c).wait_send()
+
         for stage in range(half):
             for way in range(2):
                 if span(way, stage)[1]:
@@ -250,7 +262,7 @@
             pltpu.SemaphoreType.DMA((2, half, chunks)),
         ],
         compiler_params=pltpu.CompilerParams(
-            collective_id=0, has_side_effects=True, vmem_limit_bytes=48 * 1024 * 1024
+            collective_id=0, has_side_effects=True, vmem_limit_bytes=60 * 1024 * 1024
         ),
     )(*tables(new, piece), history, filter_taps, skip_gain[None, :], gate_values)
 

time: 40.2 us -> 33.8 us (0.84)
  local copies, waits for them, and re-layouts: 6.39 us -> 1.67 us
  Pallas kernels: 33.5 us -> 31.9 us
    unnamed x13 -> x1, local copies, waits for them, and re-layouts: 6.39 us -> 1.67 us
    pallas_call x1, Pallas kernels: 33.5 us -> 31.9 us  [body(): pl.pallas_call(functools.partial(kernel, n, new, piece, width, first), ou...]
where the time goes in v2:
time: 33.8 us; the launch traced here: 33.6 us
  Pallas kernels  31.9 us (94%)
  local copies, waits for them, and re-layouts  1.67 us (5%)
    pallas_call x1, Pallas kernels, body(): pl.pallas_call(functools.partial(kernel, n, new, piece, width, first), ou...  31.9 us
    unnamed x1, local copies, waits for them, and re-layouts  1.67 us

profile of v2, /device:TPU:0, one launch (start us, length us, event | category | flops | bytes accessed | tf_op | source)
XLA Modules:
  0.0 33.6 jit_solution(17154408176121057115)
XLA Ops:
  0.0 31.9 %shard_map.73 = bf16[4,16,2048]{2,1,0:T(8,128)(2,1)} custom-call(bf16[192,192]{1,0:T(8,128)(2,1)} %constant.6.clone.ft_hbm, bf16[192,128]{1,0:T(8,128)(2,1)} %constant.7.clone.fh_hbm, bf16[64,192]{1,0:T(8,128)(2,1)} %constant.8.clone.fi_hbm, bf16[4,512,2048]{2,1,0:T(8,128)(2,1)} %hist_hbm.1, bf16[512,2048]{1,0:T(8,128)(2,1)} %taps_hbm.1, f32[1,2048]{1,0:T(1,128)} %bitcast.1, ...), custom_call_target="tpu_custom_call" | custom-call | tf_op jit(solution)/shard_map/pallas_call | solution.py:237
  31.9 1.7 %copy.9 = bf16[4,16,2048]{2,1,0:T(8,128)(2,1)} copy(bf16[4,16,2048]{2,1,0:T(8,128)(2,1)} %shard_map.73) | data formatting | bytes 524288

commit v3 on v2

--- a/solution.py
+++ b/solution.py
@@ -12,7 +12,7 @@
 MESH = pl.DeviceIdType.MESH
 F32 = jnp.float32
 BF16 = jnp.bfloat16
-LAG = 2
+LAG = 3
 
 
 def tables(new, piece):

time: 33.8 us -> 33.8 us (level)
  no operation moved by 1% of the time
where the time goes in v3:
time: 33.8 us; the launch traced here: 33.7 us
  Pallas kernels  32 us (95%)
  local copies, waits for them, and re-layouts  1.67 us (5%)
    pallas_call x1, Pallas kernels, body(): pl.pallas_call(functools.partial(kernel, n, new, piece, width, first), ou...  32 us
    unnamed x1, local copies, waits for them, and re-layouts  1.67 us

profile of v3, /device:TPU:0, one launch (start us, length us, event | category | flops | bytes accessed | tf_op | source)
XLA Modules:
  0.0 33.7 jit_solution(13447158253504401556)
XLA Ops:
  0.0 32.0 %shard_map.73 = bf16[4,16,2048]{2,1,0:T(8,128)(2,1)} custom-call(bf16[192,192]{1,0:T(8,128)(2,1)} %constant.6.clone.ft_hbm, bf16[192,128]{1,0:T(8,128)(2,1)} %constant.7.clone.fh_hbm, bf16[64,192]{1,0:T(8,128)(2,1)} %constant.8.clone.fi_hbm, bf16[4,512,2048]{2,1,0:T(8,128)(2,1)} %hist_hbm.1, bf16[512,2048]{1,0:T(8,128)(2,1)} %taps_hbm.1, f32[1,2048]{1,0:T(1,128)} %bitcast.1, ...), custom_call_target="tpu_custom_call" | custom-call | tf_op jit(solution)/shard_map/pallas_call | solution.py:237
  32.0 1.7 %copy.9 = bf16[4,16,2048]{2,1,0:T(8,128)(2,1)} copy(bf16[4,16,2048]{2,1,0:T(8,128)(2,1)} %shard_map.73) | data formatting | bytes 524288
